TPU v7x, 128 devices: a whole 4x4x4 slice. The times are simulated.
128 devices in a mesh: gx: 8 (over x, core), gy: 16 (over y, z).
Axes of the slice: x: 4, y: 4, z: 4, core: 2. Of those that a mesh axis runs over, the one named last changes fastest.
Arguments:
- tokens: bfloat16 [512, 8192], P('gy', 'gx'), may hold values from -6 to 6
- up_old: bfloat16 [32768, 8192], P(('gx', 'gy')), may hold values from -0.0625 to 0.0625
- down_old: bfloat16 [32768, 8192], P(('gx', 'gy')), may hold values from -0.0625 to 0.0625
- old_slot: int32 [256], replicated, may hold values from 0 to 255, as said below
- new_owner: int32 [256], replicated, may hold values from 0 to 127, as said below
- hot_rank: int32 [256], replicated, may hold values from 0 to 1, as said below
- route: int32 [512], replicated, may hold values from 0 to 511, each once
Outputs:
- up_new: bfloat16 [32768, 8192], P(('gx', 'gy'))
- down_new: bfloat16 [32768, 8192], P(('gx', 'gy'))
- mixed: bfloat16 [512, 8192], P('gy', 'gx')
Inputs may be any that keep to these rules, and one draw needn't show every extreme that they name: `old_slot`: each slot number appears exactly once. `new_owner`: each device index is the new owner of exactly 2 blocks. `hot_rank`: the blocks of one new owner have distinct ranks.
All inputs are finite; a program needn't handle non-finite values.
Results may differ from a plain program's by a relative error of at most 0.0049.
Values may be sent and summed in bfloat16 or wider, within the bound.
A program may use at most 128 MiB of HBM per device.

v0:
```python
import jax
import jax.numpy as jnp
from jax import lax
from jax.sharding import PartitionSpec as P

BLOCK = 128


def split_up(shard, dim, peers):
    lengths = shard.shape
    parts = shard.reshape(*lengths[:dim], peers, lengths[dim] // peers, *lengths[dim + 1 :])
    return jnp.moveaxis(parts, dim, 0)


def laid_out(parts, dim):
    parts = jnp.moveaxis(parts, 0, dim)
    lengths = parts.shape
    return parts.reshape(*lengths[:dim], lengths[dim] * lengths[dim + 1], *lengths[dim + 2 :])


def exchange_both(shard, axis, axes, splits, concats):
    sizes = [lax.axis_size(a) for a in axes]
    parts = split_up(shard, splits[0], sizes[0])
    parts = jnp.moveaxis(split_up(parts, splits[1] + 1, sizes[1]), 0, 1)
    inside = parts.shape[2:]
    parts = parts.reshape(-1, *inside)
    parts = lax.all_to_all(parts, axis, split_axis=0, concat_axis=0, tiled=True)
    parts = laid_out(parts.reshape(*sizes, *inside), concats[0] + 1)
    return laid_out(parts, concats[1])


def sum_at_owner(shard, axis, dim):
    parts = split_up(shard, dim, lax.axis_size(axis))
    arrived = lax.all_to_all(parts, axis, split_axis=0, concat_axis=0, tiled=True)
    return arrived.sum(axis=0)


def layer_terms(ordered, up_rows, down_rows):
    pre = lax.dot_general(
        ordered, up_rows, (((1,), (1,)), ((), ())), preferred_element_type=jnp.float32
    )
    hidden = jax.nn.gelu(pre, approximate=False).astype(jnp.bfloat16)
    return jnp.dot(hidden, down_rows, preferred_element_type=jnp.float32)


def relocate(up_old, down_old, old_slot, new_owner, hot_rank):
    held = up_old.shape[0] // BLOCK
    width = up_old.shape[1]
    shaped = (up_old.reshape(held, BLOCK, width), down_old.reshape(held, BLOCK, width))
    across_x = lax.axis_size("gx")
    across_y = lax.axis_size("gy")
    sectioned = (
        exchange_both(shaped[0], ("gx", "gy"), ("gx", "gy"), (1, 1), (0, 0)),
        exchange_both(shaped[1], ("gx", "gy"), ("gx", "gy"), (1, 1), (0, 0)),
    )
    share = sectioned[0].shape[1]

    def reorder(arr):
        arr = arr.reshape(across_y, across_x, held, share, width)
        return jnp.transpose(arr, (1, 0, 2, 3, 4)).reshape(across_x * across_y * held, share, width)

    spread = (reorder(sectioned[0]), reorder(sectioned[1]))
    total = spread[0].shape[0]
    new_slot = new_owner * held + hot_rank
    source = jnp.zeros((total,), jnp.int32).at[new_slot].set(old_slot)
    picked = (jnp.take(spread[0], source, axis=0), jnp.take(spread[1], source, axis=0))
    landed = (
        lax.all_to_all(picked[0], ("gx", "gy"), split_axis=0, concat_axis=1, tiled=True),
        lax.all_to_all(picked[1], ("gx", "gy"), split_axis=0, concat_axis=1, tiled=True),
    )
    return (landed[0].reshape(held * BLOCK, width), landed[1].reshape(held * BLOCK, width))


def shards(tokens, up_old, down_old, old_slot, new_owner, hot_rank, route):
    feature_rows = lax.all_gather(tokens, "gx", axis=1, tiled=True)
    everyone = lax.all_gather(feature_rows, "gy", axis=0, tiled=True)
    ordered = jnp.take(everyone, route, axis=0)
    up_new, down_new = relocate(up_old, down_old, old_slot, new_owner, hot_rank)
    partial_out = layer_terms(ordered, up_new, down_new)
    by_columns = lax.psum_scatter(partial_out, "gx", scatter_dimension=1, tiled=True)
    summed = sum_at_owner(by_columns, "gy", 0)
    return (up_new, down_new, summed.astype(jnp.bfloat16))


def solution(mesh):
    in_specs = (P("gy", "gx"), P(("gx", "gy"), None), P(("gx", "gy"), None), P(), P(), P(), P())
    out_specs = (P(("gx", "gy"), None), P(("gx", "gy"), None), P("gy", "gx"))
    return jax.shard_map(shards, mesh=mesh, in_specs=in_specs, out_specs=out_specs, check_vma=False)
```

profile of v0, /device:TPU:0, one launch (start us, length us, event | category | flops | bytes accessed | tf_op | source)
XLA Modules:
  0.0 561.5 jit_solution(2574933312884499092)
XLA Ops:
  7.2 8.6 %copy.24 = bf16[2,8,16,8192]{3,0,2,1:T(2,128)(2,1)} copy(bf16[2,8,16,8192]{3,2,1,0:T(8,128)(2,1)} %bitcast.36) | data formatting | bytes 8388608 | tf_op jit(solution)/shard_map/reshape;reshape | solution.py:11
  15.7 0.0 copy-start
  15.7 11.7 %all-to-all-start = ((bf16[128,2,1,8192]{3,1,2,0:T(2,128)(2,1)}), bf16[128,2,1,8192]{3,1,2,0:T(2,128)(2,1)}, u32[]{:S(2)}, u32[]{:S(2)}) async-start(bf16[128,2,1,8192]{3,1,2,0:T(2,128)(2,1)} %bitcast.33), calls=%async_computation | async-start | bytes 8388608 | tf_op jit(solution)/shard_map/all_to_all | solution.py:27
  27.5 0.0 all-gather.2.cloned.1.call-start
  27.5 0.0 copy-done
  27.5 55.9 %all_gather.6 = bf16[32,8192]{1,0:T(8,128)(2,1)} all-gather(bf16[32,1024]{1,0:T(8,128)(2,1)S(1)} %copy-done), channel_id=1, replica_groups=mesh['gx'=8,'gy'=16] {'gx'}, dimensions={1}, use_global_device_ids=true | all-gather | bytes 589824 | tf_op jit(solution)/shard_map/all_gather | solution.py:75
  83.5 0.0 all-gather.2.cloned.1.call-update
  83.5 8.6 %copy.27 = bf16[2,8,16,8192]{3,0,2,1:T(2,128)(2,1)} copy(bf16[2,8,16,8192]{3,2,1,0:T(8,128)(2,1)} %bitcast.37) | data formatting | bytes 8388608 | tf_op jit(solution)/shard_map/reshape;reshape | solution.py:11
  92.1 0.0 all-to-all-done
  92.1 0.0 copy-start.2
  92.1 0.0 copy-start.3
  92.1 10.7 %all-to-all-start.2 = ((bf16[128,2,1,8192]{3,1,2,0:T(2,128)(2,1)}), bf16[128,2,1,8192]{3,1,2,0:T(2,128)(2,1)}, u32[]{:S(2)}, u32[]{:S(2)}) async-start(bf16[128,2,1,8192]{3,1,2,0:T(2,128)(2,1)} %bitcast.32), calls=%async_computation.2 | async-start | bytes 8388608 | tf_op jit(solution)/shard_map/all_to_all | solution.py:27
  102.8 0.0 copy-done.2
  102.8 0.0 copy-done.3
  102.8 1.6 scatter_custom_fusion
  104.4 7.2 %reshape.111 = bf16[256,8192]{1,0:T(8,128)(2,1)} reshape(bf16[128,2,1,8192]{3,1,2,0:T(2,128)(2,1)} %all-to-all-done) | data formatting | bytes 8388608 | tf_op jit(solution)/shard_map/jit(_take)/Arg_0.7 | solution.py:66
  111.6 11.7 %gather_fusion.1 = bf16[256,8192]{1,0:T(8,128)(2,1)} fusion(bf16[256,8192]{1,0:T(8,128)(2,1)} %reshape.111, s32[1024]{0:T(1024)S(1)} %pad_clamp_fusion.1), kind=kCustom, calls=%fused_computation.clone | custom fusion | bytes 8389632 | tf_op jit(solution)/shard_map/jit(_take)/gather | solution.py:66
  123.3 32.9 %all-to-all-done.2 = bf16[128,2,1,8192]{3,1,2,0:T(2,128)(2,1)} async-done(((bf16[128,2,1,8192]{3,1,2,0:T(2,128)(2,1)}), bf16[128,2,1,8192]{3,1,2,0:T(2,128)(2,1)}, u32[]{:S(2)}, u32[]{:S(2)}) %all-to-all-start.2) | async-done | bytes 4194336 | tf_op jit(solution)/shard_map/all_to_all | solution.py:27
  156.3 7.7 %reshape.115 = bf16[256,8192]{1,0:T(8,128)(2,1)} reshape(bf16[128,2,1,8192]{3,1,2,0:T(2,128)(2,1)} %all-to-all-done.2) | data formatting | bytes 8388608 | tf_op jit(solution)/shard_map/jit(_take)/Arg_0.7 | solution.py:66
  164.0 11.7 %gather_fusion.2 = bf16[256,8192]{1,0:T(8,128)(2,1)} fusion(bf16[256,8192]{1,0:T(8,128)(2,1)} %reshape.115, s32[1024]{0:T(1024)S(1)} %pad_clamp_fusion.1), kind=kCustom, calls=%fused_computation.1.clone | custom fusion | bytes 8389632 | tf_op jit(solution)/shard_map/jit(_take)/gather | solution.py:66
  175.7 6.0 %bitcast_select_fusion = (bf16[256,1,8192]{2,0,1:T(8,128)(2,1)}, bf16[256,1,8192]{2,0,1:T(8,128)(2,1)}) fusion(bf16[256,8192]{1,0:T(8,128)(2,1)} %gather_fusion.2, pred[256]{0:T(512)(128)(4,1)S(1)} %compare_and_fusion, bf16[256,8192]{1,0:T(8,128)(2,1)} %gather_fusion.1), kind=kLoop, calls=%fused_computation.7 | loop fusion | flops 4194304 | bytes 16777472 | tf_op jit(solution)/shard_map/jit(_take)/select_n | solution.py:66
  181.8 0.5 broadcast.59
  182.3 6.8 %reduce.2 = bf16[256,8192]{1,0:T(8,128)(2,1)} reduce(bf16[256,1,8192]{2,0,1:T(8,128)(2,1)} %get-tuple-element.5, bf16[]{:T(256)} %broadcast.59), dimensions={1}, to_apply=%copy.25.reduce_sub_computation | reduce | bytes 8388610 | tf_op jit(solution)/shard_map/jit(_take)/select_n | solution.py:66
  189.1 7.6 %reshape.125 = bf16[128,2,8192]{2,1,0:T(2,128)(2,1)} reshape(bf16[256,8192]{1,0:T(8,128)(2,1)} %reduce.2) | data formatting | bytes 8388608
  196.7 7.7 %all-to-all-start.1 = ((bf16[128,2,8192]{2,1,0:T(2,128)(2,1)}), bf16[128,2,8192]{2,1,0:T(2,128)(2,1)}, u32[]{:S(2)}, u32[]{:S(2)}) async-start(bf16[128,2,8192]{2,1,0:T(2,128)(2,1)} %reshape.125), calls=%async_computation.1 | async-start | bytes 8388608 | tf_op jit(solution)/shard_map/all_to_all | solution.py:68
  204.5 6.7 %reduce.3 = bf16[256,8192]{1,0:T(8,128)(2,1)} reduce(bf16[256,1,8192]{2,0,1:T(8,128)(2,1)} %get-tuple-element.4, bf16[]{:T(256)} %broadcast.59), dimensions={1}, to_apply=%copy.28.reduce_sub_computation | reduce | bytes 8388610 | tf_op jit(solution)/shard_map/jit(_take)/select_n | solution.py:66
  211.2 7.6 %reshape.127 = bf16[128,2,8192]{2,1,0:T(2,128)(2,1)} reshape(bf16[256,8192]{1,0:T(8,128)(2,1)} %reduce.3) | data formatting | bytes 8388608
  218.8 0.0 copy-start.1
  218.8 38.0 %all-to-all-done.1 = bf16[128,2,8192]{2,1,0:T(2,128)(2,1)} async-done(((bf16[128,2,8192]{2,1,0:T(2,128)(2,1)}), bf16[128,2,8192]{2,1,0:T(2,128)(2,1)}, u32[]{:S(2)}, u32[]{:S(2)}) %all-to-all-start.1) | async-done | bytes 4194336 | tf_op jit(solution)/shard_map/all_to_all | solution.py:68
  256.8 5.8 %all-to-all-start.3 = ((bf16[128,2,8192]{2,1,0:T(2,128)(2,1)}), bf16[128,2,8192]{2,1,0:T(2,128)(2,1)}, u32[]{:S(2)}, u32[]{:S(2)}) async-start(bf16[128,2,8192]{2,1,0:T(2,128)(2,1)} %reshape.127), calls=%async_computation.3 | async-start | bytes 8388608 | tf_op jit(solution)/shard_map/all_to_all | solution.py:69
  262.6 0.0 reduce-scatter.2.cloned.1.call-start
  262.7 0.0 copy-done.1
  262.7 19.8 %reshape.126 = bf16[256,1,8192]{2,1,0:T(2,128)(2,1)} reshape(bf16[128,2,8192]{2,1,0:T(2,128)(2,1)} %all-to-all-done.1) | data formatting | bytes 8388608
  282.5 26.3 %reduce = bf16[256,8192]{1,0:T(8,128)(2,1)} reduce(bf16[256,1,8192]{2,1,0:T(2,128)(2,1)} %reshape.126, bf16[]{:T(256)} %constant.92), dimensions={1}, to_apply=%all_to_all.32.reduce_sub_computation | reduce | bytes 8388610 | tf_op jit(solution)/shard_map/all_to_all | solution.py:68
  308.7 7.7 %all_to_all.33 = bf16[128,2,1,8192]{3,1,0,2:T(2,128)(2,1)} reshape(bf16[256,8192]{1,0:T(8,128)(2,1)} %reduce) | data formatting | bytes 8388608 | tf_op jit(solution)/shard_map/all_to_all | solution.py:68
  316.4 6.9 %copy.26 = bf16[2,128,1,8192]{3,1,0,2:T(8,128)(2,1)} copy(bf16[2,128,1,8192]{3,0,1,2:T(2,128)(2,1)} %bitcast.34) | data formatting | bytes 8388608 | tf_op jit(solution)/shard_map/all_to_all | solution.py:68
  323.3 0.0 all-to-all-done.3
  323.3 19.8 %reshape.128 = bf16[256,1,8192]{2,1,0:T(2,128)(2,1)} reshape(bf16[128,2,8192]{2,1,0:T(2,128)(2,1)} %all-to-all-done.3) | data formatting | bytes 8388608
  343.1 26.3 %reduce.1 = bf16[256,8192]{1,0:T(8,128)(2,1)} reduce(bf16[256,1,8192]{2,1,0:T(2,128)(2,1)} %reshape.128, bf16[]{:T(256)} %constant.92), dimensions={1}, to_apply=%all_to_all.36.reduce_sub_computation | reduce | bytes 8388610 | tf_op jit(solution)/shard_map/all_to_all | solution.py:69
  369.3 7.9 %all_to_all.37 = bf16[128,2,1,8192]{3,1,0,2:T(2,128)(2,1)} reshape(bf16[256,8192]{1,0:T(8,128)(2,1)} %reduce.1) | data formatting | bytes 8388608 | tf_op jit(solution)/shard_map/all_to_all | solution.py:69
  377.2 6.9 %copy.29 = bf16[2,128,1,8192]{3,1,0,2:T(8,128)(2,1)} copy(bf16[2,128,1,8192]{3,0,1,2:T(2,128)(2,1)} %bitcast.35) | data formatting | bytes 8388608 | tf_op jit(solution)/shard_map/all_to_all | solution.py:69
  384.1 0.0 all-gather.2.cloned.1.call-done
  384.1 20.2 %gather_fusion = bf16[512,8192]{1,0:T(8,128)(2,1)} fusion(bf16[512,8192]{1,0:T(8,128)(2,1)} %all-gather.2.cloned.1.call-done, s32[1024]{0:T(1024)S(1)} %pad_clamp_fusion), kind=kCustom, calls=%fused_computation.2 | custom fusion | bytes 16779264 | tf_op jit(solution)/shard_map/jit(_take)/gather | solution.py:77
  404.3 21.5 %fusion.17 = f32[512,8192]{1,0:T(8,128)} fusion(bf16[256,8192]{1,0:T(8,128)(2,1)} %bitcast.40, bf16[256,8192]{1,0:T(8,128)(2,1)} %bitcast.38, bf16[512,8192]{1,0:T(8,128)(2,1)} %gather_fusion, pred[512]{0:T(512)(128)(4,1)S(1)} %compare_and_fusion.1), kind=kOutput, calls=%fused_computation.29 | convolution fusion | flops 4307681280 | bytes 33554944 | tf_op jit(solution)/shard_map/dot_general | solution.py:43
  425.7 0.0 reduce-scatter.2.cloned.1.call-update
  425.8 92.9 %reduce-scatter.2.cloned.1.call-done = f32[512,1024]{1,0:T(8,128)} async-done(((f32[512,8192]{1,0:T(8,128)}), f32[512,1024]{1,0:T(8,128)}) %reduce-scatter.2.cloned.1.call-update) | async-done | bytes 2097168 | tf_op jit(solution)/shard_map/reduce_scatter | solution.py:80
  518.6 34.8 %all_to_all.45 = f32[16,32,1024]{2,1,0:T(8,128)S(1)} all-to-all(f32[16,32,1024]{2,1,0:T(8,128)} %bitcast.42), channel_id=1, replica_groups=mesh['gx'=8,'gy'=16] {'gy'}, dimensions={0} | all-to-all | bytes 4194304 | tf_op jit(solution)/shard_map/all_to_all | solution.py:34
  553.5 0.7 reduce_sum.9
  (7 shorter events, 0.0 us)
Async XLA Ops:
  15.7 11.8 %copy-start = (bf16[32,1024]{1,0:T(8,128)(2,1)S(1)}, bf16[32,1024]{1,0:T(8,128)(2,1)}, u32[]{:S(2)}) copy-start(bf16[32,1024]{1,0:T(8,128)(2,1)} %param.9) | copy-start | bytes 196612
  15.7 76.3 %all-to-all-start = ((bf16[128,2,1,8192]{3,1,2,0:T(2,128)(2,1)}), bf16[128,2,1,8192]{3,1,2,0:T(2,128)(2,1)}, u32[]{:S(2)}, u32[]{:S(2)}) async-start(bf16[128,2,1,8192]{3,1,2,0:T(2,128)(2,1)} %bitcast.33), calls=%async_computation | async-start | bytes 8388608 | tf_op jit(solution)/shard_map/all_to_all | solution.py:27
  27.5 356.7 %all-gather.2.cloned.1.call-start = ((), (), s32[]{:S(2)}) async-start(), calls=%async_computation.6 | async-start | bytes 8912896 | tf_op jit(solution)/shard_map/all_gather | solution.py:76
  92.1 10.8 %copy-start.2 = (s32[256]{0:T(256)S(1)}, s32[256]{0:T(256)}, u32[]{:S(2)}) copy-start(s32[256]{0:T(256)} %param.14) | copy-start | bytes 3076
  92.1 10.8 %copy-start.3 = (s32[256]{0:T(256)S(1)}, s32[256]{0:T(256)}, u32[]{:S(2)}) copy-start(s32[256]{0:T(256)} %param.13) | copy-start | bytes 3076
  92.1 64.2 %all-to-all-start.2 = ((bf16[128,2,1,8192]{3,1,2,0:T(2,128)(2,1)}), bf16[128,2,1,8192]{3,1,2,0:T(2,128)(2,1)}, u32[]{:S(2)}, u32[]{:S(2)}) async-start(bf16[128,2,1,8192]{3,1,2,0:T(2,128)(2,1)} %bitcast.32), calls=%async_computation.2 | async-start | bytes 8388608 | tf_op jit(solution)/shard_map/all_to_all | solution.py:27
  196.7 60.0 %all-to-all-start.1 = ((bf16[128,2,8192]{2,1,0:T(2,128)(2,1)}), bf16[128,2,8192]{2,1,0:T(2,128)(2,1)}, u32[]{:S(2)}, u32[]{:S(2)}) async-start(bf16[128,2,8192]{2,1,0:T(2,128)(2,1)} %reshape.125), calls=%async_computation.1 | async-start | bytes 8388608 | tf_op jit(solution)/shard_map/all_to_all | solution.py:68
  218.8 43.8 %copy-start.1 = (s32[512]{0:T(512)S(1)}, s32[512]{0:T(512)}, u32[]{:S(2)}) copy-start(s32[512]{0:T(512)} %param.15) | copy-start | bytes 6148
  256.8 66.5 %all-to-all-start.3 = ((bf16[128,2,8192]{2,1,0:T(2,128)(2,1)}), bf16[128,2,8192]{2,1,0:T(2,128)(2,1)}, u32[]{:S(2)}, u32[]{:S(2)}) async-start(bf16[128,2,8192]{2,1,0:T(2,128)(2,1)} %reshape.127), calls=%async_computation.3 | async-start | bytes 8388608 | tf_op jit(solution)/shard_map/all_to_all | solution.py:69
  262.6 256.0 %reduce-scatter.2.cloned.1.call-start = ((), (), s32[]{:S(2)}) async-start(), calls=%async_computation.7 | async-start | bytes 18874368 | tf_op jit(solution)/shard_map/reduce_scatter | solution.py:80
Sparse Core Ops, SparseCore 0:
  83.6 115.8 all-gather.1
  425.9 92.7 reduce-scatter.1
where the time goes:
time: 572 us; the launch traced here: 561 us
  waiting for transfers between devices  164 us (29%)
  local copies, waits for them, and re-layouts  162 us (28%)
  blocking collectives  90.8 us (16%)
  other arithmetic  72.9 us (13%)
  starting transfers between devices  36.1 us (6%)
  matrix products  21.5 us (4%)
  between operations  14.6 us (3%)
    reduce_scatter x1, waiting for transfers between devices, shards(): lax.psum_scatter(partial_out, 'gx', scatter_dimension=1, tiled=True)  92.9 us
    all_gather x1, blocking collectives, shards(): feature_rows = lax.all_gather(tokens, 'gx', axis=1, tiled=True)  55.9 us
    unnamed x12, local copies, waits for them, and re-layouts  54.8 us
    all_to_all x1, waiting for transfers between devices, relocate(): lax.all_to_all(picked[0], ('gx', 'gy'), split_axis=0, concat_axis=1, tile...  38 us
    all_to_all x1, blocking collectives, sum_at_owner(): lax.all_to_all(parts, axis, split_axis=0, concat_axis=0, tiled=True)  34.8 us
    all_to_all x2, waiting for transfers between devices, exchange_both(): parts = lax.all_to_all(parts, axis, split_axis=0, concat_axis=0, tiled=True)  32.9 us
    all_to_all x1, other arithmetic, relocate(): lax.all_to_all(picked[0], ('gx', 'gy'), split_axis=0, concat_axis=1, tile...  26.3 us
    all_to_all x1, other arithmetic, relocate(): lax.all_to_all(picked[1], ('gx', 'gy'), split_axis=0, concat_axis=1, tile...  26.3 us
  transfers between devices with their start and end apart: 6, of which 3 were waited for; matrix products, arithmetic and copies ran while one was open for 34% of the time, Pallas kernels for 0%

commit v1 on v0

--- a/solution.py
+++ b/solution.py
@@ -4,6 +4,12 @@
 from jax.sharding import PartitionSpec as P
 
 BLOCK = 128
+
+
+def in_order(blocks, dim):
+    blocks = jnp.moveaxis(blocks, 0, dim)
+    shape = blocks.shape
+    return blocks.reshape(*shape[:dim], shape[dim] * shape[dim + 1], *shape[dim + 2 :])
 
 
 def split_up(shard, dim, peers):
@@ -72,7 +78,19 @@
 
 
 def shards(tokens, up_old, down_old, old_slot, new_owner, hot_rank, route):
-    feature_rows = lax.all_gather(tokens, "gx", axis=1, tiled=True)
+    length = lax.axis_size("gx")
+    pairs = [(i, (i + 1) % length) for i in range(length)]
+    back = [(b, a_2) for a_2, b in pairs]
+    lower, upper = ([], [])
+    for step in range(length - 1):
+        if step % 2 == 0:
+            lower.append(lax.ppermute(lower[-1] if lower else tokens, "gx", pairs))
+        else:
+            upper.append(lax.ppermute(upper[-1] if upper else tokens, "gx", back))
+    blocks = jnp.stack([*lower[::-1], tokens, *upper])
+    shift = lax.axis_index("gx") - len(lower)
+    blocks = blocks[(jnp.arange(length) - shift) % length]
+    feature_rows = in_order(blocks, 1)
     everyone = lax.all_gather(feature_rows, "gy", axis=0, tiled=True)
     ordered = jnp.take(everyone, route, axis=0)
     up_new, down_new = relocate(up_old, down_old, old_slot, new_owner, hot_rank)

time: 572 us -> 580 us (1.014)
  blocking collectives: 90.8 us -> 34.8 us
  waiting for transfers between devices: 164 us -> 217 us
  starting transfers between devices: 36.1 us -> 45.1 us
    all_gather x1 -> x0, blocking collectives: 55.9 us -> none  [shards(): feature_rows = lax.all_gather(tokens, 'gx', axis=1, tiled=True)]
    ppermute x0 -> x7, waiting for transfers between devices: none -> 53.3 us  [the longest x4 53.3 us: shards(): lower.append(lax.ppermute(lower[-1] if lower else tokens, 'gx', pairs))]
    ppermute x0 -> x7, starting transfers between devices: none -> 8.91 us  [the longest x3 8.88 us: shards(): upper.append(lax.ppermute(upper[-1] if upper else tokens, 'gx', back))]
    unnamed x12 -> x19, local copies, waits for them, and re-layouts: 54.8 us -> 55 us
  transfers between devices with their start and end apart: 6 -> 13, of which waited for: 3 -> 7; matrix products, arithmetic and copies ran while one was open for 34% -> 34% of each run, Pallas kernels for 0% -> 0%
where the time goes in v1:
time: 580 us; the launch traced here: 570 us
  waiting for transfers between devices  217 us (37%)
  local copies, waits for them, and re-layouts  163 us (28%)
  other arithmetic  72.9 us (13%)
  starting transfers between devices  45.1 us (8%)
  blocking collectives  34.8 us (6%)
  matrix products  21.5 us (4%)
  between operations  14.7 us (3%)
    reduce_scatter x1, waiting for transfers between devices, shards(): lax.psum_scatter(partial_out, 'gx', scatter_dimension=1, tiled=True)  92.9 us
    unnamed x19, local copies, waits for them, and re-layouts  55 us
    ppermute x4, waiting for transfers between devices, shards(): lower.append(lax.ppermute(lower[-1] if lower else tokens, 'gx', pairs))  53.3 us
    all_to_all x1, waiting for transfers between devices, relocate(): lax.all_to_all(picked[0], ('gx', 'gy'), split_axis=0, concat_axis=1, tile...  37.9 us
    all_to_all x1, blocking collectives, sum_at_owner(): lax.all_to_all(parts, axis, split_axis=0, concat_axis=0, tiled=True)  34.8 us
    all_to_all x2, waiting for transfers between devices, exchange_both(): parts = lax.all_to_all(parts, axis, split_axis=0, concat_axis=0, tiled=True)  33 us
    all_to_all x1, other arithmetic, relocate(): lax.all_to_all(picked[0], ('gx', 'gy'), split_axis=0, concat_axis=1, tile...  26.3 us
    all_to_all x1, other arithmetic, relocate(): lax.all_to_all(picked[1], ('gx', 'gy'), split_axis=0, concat_axis=1, tile...  26.3 us
  transfers between devices with their start and end apart: 13, of which 7 were waited for; matrix products, arithmetic and copies ran while one was open for 34% of the time, Pallas kernels for 0%

profile of v1, /device:TPU:0, one launch (start us, length us, event | category | flops | bytes accessed | tf_op | source)
XLA Modules:
  0.0 569.6 jit_solution(2346135480247703663)
XLA Ops:
  7.2 8.6 %copy.27 = bf16[2,8,16,8192]{3,0,2,1:T(2,128)(2,1)} copy(bf16[2,8,16,8192]{3,2,1,0:T(8,128)(2,1)} %bitcast.57) | data formatting | bytes 8388608 | tf_op jit(solution)/shard_map/reshape;reshape | solution.py:17
  15.7 11.7 %all-to-all-start = ((bf16[128,2,1,8192]{3,1,2,0:T(2,128)(2,1)}), bf16[128,2,1,8192]{3,1,2,0:T(2,128)(2,1)}, u32[]{:S(2)}, u32[]{:S(2)}) async-start(bf16[128,2,1,8192]{3,1,2,0:T(2,128)(2,1)} %bitcast.53), calls=%async_computation | async-start | bytes 8388608 | tf_op jit(solution)/shard_map/all_to_all | solution.py:33
  27.5 0.0 all-gather.2.cloned.1.call-start
  27.5 0.0 collective-permute-start
  27.5 47.5 %collective-permute-done = bf16[32,1024]{1,0:T(8,128)(2,1)S(1)} collective-permute-done((bf16[32,1024]{1,0:T(8,128)(2,1)S(1)}, bf16[32,1024]{1,0:T(8,128)(2,1)S(1)}, u32[]{:S(2)}, u32[]{:S(2)}) %collective-permute-start) | collective-permute-done | bytes 65568 | tf_op jit(solution)/shard_map/ppermute | solution.py:87
  75.0 3.0 collective-permute-start.4
  78.0 1.9 collective-permute-done.1
  79.9 0.0 collective-permute-start.2
  80.0 3.0 collective-permute-start.5
  82.9 1.9 collective-permute-done.2
  84.8 0.0 collective-permute-start.3
  84.9 3.0 collective-permute-start.6
  87.8 1.9 collective-permute-done.3
  89.9 0.6 gather_fusion
  90.4 0.9 copy.36
  91.3 0.0 all-gather.2.cloned.1.call-update
  91.3 8.6 %copy.30 = bf16[2,8,16,8192]{3,0,2,1:T(2,128)(2,1)} copy(bf16[2,8,16,8192]{3,2,1,0:T(8,128)(2,1)} %bitcast.58) | data formatting | bytes 8388608 | tf_op jit(solution)/shard_map/reshape;reshape | solution.py:17
  99.9 10.9 %all-to-all-start.2 = ((bf16[128,2,1,8192]{3,1,2,0:T(2,128)(2,1)}), bf16[128,2,1,8192]{3,1,2,0:T(2,128)(2,1)}, u32[]{:S(2)}, u32[]{:S(2)}) async-start(bf16[128,2,1,8192]{3,1,2,0:T(2,128)(2,1)} %bitcast.54), calls=%async_computation.2 | async-start | bytes 8388608 | tf_op jit(solution)/shard_map/all_to_all | solution.py:33
  110.9 1.6 scatter_custom_fusion
  112.5 7.2 %reshape.172 = bf16[256,8192]{1,0:T(8,128)(2,1)} reshape(bf16[128,2,1,8192]{3,1,2,0:T(2,128)(2,1)} %all-to-all-done) | data formatting | bytes 8388608 | tf_op jit(solution)/shard_map/jit(_take)/Arg_0.11 | solution.py:72
  119.6 11.7 %gather_fusion.2 = bf16[256,8192]{1,0:T(8,128)(2,1)} fusion(bf16[256,8192]{1,0:T(8,128)(2,1)} %reshape.172, s32[1024]{0:T(1024)S(1)} %pad_clamp_fusion.2), kind=kCustom, calls=%fused_computation.clone | custom fusion | bytes 8389632 | tf_op jit(solution)/shard_map/jit(_take)/gather | solution.py:72
  131.3 33.0 %all-to-all-done.2 = bf16[128,2,1,8192]{3,1,2,0:T(2,128)(2,1)} async-done(((bf16[128,2,1,8192]{3,1,2,0:T(2,128)(2,1)}), bf16[128,2,1,8192]{3,1,2,0:T(2,128)(2,1)}, u32[]{:S(2)}, u32[]{:S(2)}) %all-to-all-start.2) | async-done | bytes 4194336 | tf_op jit(solution)/shard_map/all_to_all | solution.py:33
  164.4 7.7 %reshape.176 = bf16[256,8192]{1,0:T(8,128)(2,1)} reshape(bf16[128,2,1,8192]{3,1,2,0:T(2,128)(2,1)} %all-to-all-done.2) | data formatting | bytes 8388608 | tf_op jit(solution)/shard_map/jit(_take)/Arg_0.11 | solution.py:72
  172.1 11.7 %gather_fusion.3 = bf16[256,8192]{1,0:T(8,128)(2,1)} fusion(bf16[256,8192]{1,0:T(8,128)(2,1)} %reshape.176, s32[1024]{0:T(1024)S(1)} %pad_clamp_fusion.2), kind=kCustom, calls=%fused_computation.1.clone | custom fusion | bytes 8389632 | tf_op jit(solution)/shard_map/jit(_take)/gather | solution.py:72
  183.8 6.0 %bitcast_select_fusion = (bf16[256,1,8192]{2,0,1:T(8,128)(2,1)}, bf16[256,1,8192]{2,0,1:T(8,128)(2,1)}) fusion(bf16[256,8192]{1,0:T(8,128)(2,1)} %gather_fusion.3, pred[256]{0:T(512)(128)(4,1)S(1)} %compare_and_fusion, bf16[256,8192]{1,0:T(8,128)(2,1)} %gather_fusion.2), kind=kLoop, calls=%fused_computation.8 | loop fusion | flops 4194304 | bytes 16777472 | tf_op jit(solution)/shard_map/jit(_take)/select_n | solution.py:72
  189.8 0.5 broadcast.128
  190.4 6.8 %reduce.2 = bf16[256,8192]{1,0:T(8,128)(2,1)} reduce(bf16[256,1,8192]{2,0,1:T(8,128)(2,1)} %get-tuple-element.5, bf16[]{:T(256)} %broadcast.128), dimensions={1}, to_apply=%copy.28.reduce_sub_computation | reduce | bytes 8388610 | tf_op jit(solution)/shard_map/jit(_take)/select_n | solution.py:72
  197.2 7.6 %reshape.186 = bf16[128,2,8192]{2,1,0:T(2,128)(2,1)} reshape(bf16[256,8192]{1,0:T(8,128)(2,1)} %reduce.2) | data formatting | bytes 8388608
  204.8 7.7 %all-to-all-start.1 = ((bf16[128,2,8192]{2,1,0:T(2,128)(2,1)}), bf16[128,2,8192]{2,1,0:T(2,128)(2,1)}, u32[]{:S(2)}, u32[]{:S(2)}) async-start(bf16[128,2,8192]{2,1,0:T(2,128)(2,1)} %reshape.186), calls=%async_computation.1 | async-start | bytes 8388608 | tf_op jit(solution)/shard_map/all_to_all | solution.py:74
  212.5 6.7 %reduce.3 = bf16[256,8192]{1,0:T(8,128)(2,1)} reduce(bf16[256,1,8192]{2,0,1:T(8,128)(2,1)} %get-tuple-element.4, bf16[]{:T(256)} %broadcast.128), dimensions={1}, to_apply=%copy.31.reduce_sub_computation | reduce | bytes 8388610 | tf_op jit(solution)/shard_map/jit(_take)/select_n | solution.py:72
  219.2 7.7 %reshape.188 = bf16[128,2,8192]{2,1,0:T(2,128)(2,1)} reshape(bf16[256,8192]{1,0:T(8,128)(2,1)} %reduce.3) | data formatting | bytes 8388608
  226.9 37.9 %all-to-all-done.1 = bf16[128,2,8192]{2,1,0:T(2,128)(2,1)} async-done(((bf16[128,2,8192]{2,1,0:T(2,128)(2,1)}), bf16[128,2,8192]{2,1,0:T(2,128)(2,1)}, u32[]{:S(2)}, u32[]{:S(2)}) %all-to-all-start.1) | async-done | bytes 4194336 | tf_op jit(solution)/shard_map/all_to_all | solution.py:74
  264.8 5.8 %all-to-all-start.3 = ((bf16[128,2,8192]{2,1,0:T(2,128)(2,1)}), bf16[128,2,8192]{2,1,0:T(2,128)(2,1)}, u32[]{:S(2)}, u32[]{:S(2)}) async-start(bf16[128,2,8192]{2,1,0:T(2,128)(2,1)} %reshape.188), calls=%async_computation.3 | async-start | bytes 8388608 | tf_op jit(solution)/shard_map/all_to_all | solution.py:75
  270.6 0.0 reduce-scatter.2.cloned.1.call-start
  270.7 19.8 %reshape.187 = bf16[256,1,8192]{2,1,0:T(2,128)(2,1)} reshape(bf16[128,2,8192]{2,1,0:T(2,128)(2,1)} %all-to-all-done.1) | data formatting | bytes 8388608
  290.5 26.3 %reduce = bf16[256,8192]{1,0:T(8,128)(2,1)} reduce(bf16[256,1,8192]{2,1,0:T(2,128)(2,1)} %reshape.187, bf16[]{:T(256)} %constant.117), dimensions={1}, to_apply=%all_to_all.32.reduce_sub_computation | reduce | bytes 8388610 | tf_op jit(solution)/shard_map/all_to_all | solution.py:74
  316.8 7.7 %all_to_all.33 = bf16[128,2,1,8192]{3,1,0,2:T(2,128)(2,1)} reshape(bf16[256,8192]{1,0:T(8,128)(2,1)} %reduce) | data formatting | bytes 8388608 | tf_op jit(solution)/shard_map/all_to_all | solution.py:74
  324.5 6.9 %copy.29 = bf16[2,128,1,8192]{3,1,0,2:T(8,128)(2,1)} copy(bf16[2,128,1,8192]{3,0,1,2:T(2,128)(2,1)} %bitcast.55) | data formatting | bytes 8388608 | tf_op jit(solution)/shard_map/all_to_all | solution.py:74
  331.4 19.8 %reshape.189 = bf16[256,1,8192]{2,1,0:T(2,128)(2,1)} reshape(bf16[128,2,8192]{2,1,0:T(2,128)(2,1)} %all-to-all-done.3) | data formatting | bytes 8388608
  351.2 26.3 %reduce.1 = bf16[256,8192]{1,0:T(8,128)(2,1)} reduce(bf16[256,1,8192]{2,1,0:T(2,128)(2,1)} %reshape.189, bf16[]{:T(256)} %constant.117), dimensions={1}, to_apply=%all_to_all.36.reduce_sub_computation | reduce | bytes 8388610 | tf_op jit(solution)/shard_map/all_to_all | solution.py:75
  377.4 7.9 %all_to_all.37 = bf16[128,2,1,8192]{3,1,0,2:T(2,128)(2,1)} reshape(bf16[256,8192]{1,0:T(8,128)(2,1)} %reduce.1) | data formatting | bytes 8388608 | tf_op jit(solution)/shard_map/all_to_all | solution.py:75
  385.3 6.9 %copy.32 = bf16[2,128,1,8192]{3,1,0,2:T(8,128)(2,1)} copy(bf16[2,128,1,8192]{3,0,1,2:T(2,128)(2,1)} %bitcast.56) | data formatting | bytes 8388608 | tf_op jit(solution)/shard_map/all_to_all | solution.py:75
  392.2 20.2 %gather_fusion.1 = bf16[512,8192]{1,0:T(8,128)(2,1)} fusion(bf16[512,8192]{1,0:T(8,128)(2,1)} %all-gather.2.cloned.1.call-done, s32[1024]{0:T(1024)S(1)} %pad_clamp_fusion), kind=kCustom, calls=%fused_computation.3 | custom fusion | bytes 16779264 | tf_op jit(solution)/shard_map/jit(_take)/gather | solution.py:95
  412.4 21.5 %fusion.17 = f32[512,8192]{1,0:T(8,128)} fusion(bf16[256,8192]{1,0:T(8,128)(2,1)} %bitcast.61, bf16[256,8192]{1,0:T(8,128)(2,1)} %bitcast.59, bf16[512,8192]{1,0:T(8,128)(2,1)} %gather_fusion.1, pred[512]{0:T(512)(128)(4,1)S(1)} %compare_and_fusion.1), kind=kOutput, calls=%fused_computation.30 | convolution fusion | flops 4307681280 | bytes 33554944 | tf_op jit(solution)/shard_map/dot_general | solution.py:49
  433.8 0.0 reduce-scatter.2.cloned.1.call-update
  433.9 92.9 %reduce-scatter.2.cloned.1.call-done = f32[512,1024]{1,0:T(8,128)} async-done(((f32[512,8192]{1,0:T(8,128)}), f32[512,1024]{1,0:T(8,128)}) %reduce-scatter.2.cloned.1.call-update) | async-done | bytes 2097168 | tf_op jit(solution)/shard_map/reduce_scatter | solution.py:98
  526.7 34.8 %all_to_all.45 = f32[16,32,1024]{2,1,0:T(8,128)S(1)} all-to-all(f32[16,32,1024]{2,1,0:T(8,128)} %bitcast.63), channel_id=1, replica_groups=mesh['gx'=8,'gy'=16] {'gy'}, dimensions={0} | all-to-all | bytes 4194304 | tf_op jit(solution)/shard_map/all_to_all | solution.py:40
  561.6 0.7 reduce_sum.9
  (32 shorter events, 0.1 us)
Async XLA Ops:
  15.7 11.8 %copy-start = (bf16[32,1024]{1,0:T(8,128)(2,1)S(1)}, bf16[32,1024]{1,0:T(8,128)(2,1)}, u32[]{:S(2)}) copy-start(bf16[32,1024]{1,0:T(8,128)(2,1)} %param.9) | copy-start | bytes 196612
  15.7 84.2 %all-to-all-start = ((bf16[128,2,1,8192]{3,1,2,0:T(2,128)(2,1)}), bf16[128,2,1,8192]{3,1,2,0:T(2,128)(2,1)}, u32[]{:S(2)}, u32[]{:S(2)}) async-start(bf16[128,2,1,8192]{3,1,2,0:T(2,128)(2,1)} %bitcast.53), calls=%async_computation | async-start | bytes 8388608 | tf_op jit(solution)/shard_map/all_to_all | solution.py:33
  27.5 364.7 %all-gather.2.cloned.1.call-start = ((), (), s32[]{:S(2)}) async-start(), calls=%async_computation.6 | async-start | bytes 8912896 | tf_op jit(solution)/shard_map/all_gather | solution.py:94
  27.5 47.5 %collective-permute-start = (bf16[32,1024]{1,0:T(8,128)(2,1)S(1)}, bf16[32,1024]{1,0:T(8,128)(2,1)S(1)}, u32[]{:S(2)}, u32[]{:S(2)}) collective-permute-start(bf16[32,1024]{1,0:T(8,128)(2,1)S(1)} %copy-done), channel_id=1, source_target_pairs={{0,16},{16,32},{32,48},{48,64},{64,80},{80,96},{96,112},{112,0},{1... | collective-permute-start | bytes 196616 | tf_op jit(solution)/shard_map/ppermute | solution.py:87
  75.0 4.9 collective-permute-start.1
  75.0 4.9 collective-permute-start.4
  79.9 4.9 collective-permute-start.2
  80.0 4.9 collective-permute-start.5
  84.8 4.9 collective-permute-start.3
  84.9 5.0 collective-permute-start.6
  99.9 10.9 %copy-start.2 = (s32[256]{0:T(256)S(1)}, s32[256]{0:T(256)}, u32[]{:S(2)}) copy-start(s32[256]{0:T(256)} %param.14) | copy-start | bytes 3076
  99.9 10.9 %copy-start.3 = (s32[256]{0:T(256)S(1)}, s32[256]{0:T(256)}, u32[]{:S(2)}) copy-start(s32[256]{0:T(256)} %param.13) | copy-start | bytes 3076
  99.9 64.4 %all-to-all-start.2 = ((bf16[128,2,1,8192]{3,1,2,0:T(2,128)(2,1)}), bf16[128,2,1,8192]{3,1,2,0:T(2,128)(2,1)}, u32[]{:S(2)}, u32[]{:S(2)}) async-start(bf16[128,2,1,8192]{3,1,2,0:T(2,128)(2,1)} %bitcast.54), calls=%async_computation.2 | async-start | bytes 8388608 | tf_op jit(solution)/shard_map/all_to_all | solution.py:33
  204.8 60.0 %all-to-all-start.1 = ((bf16[128,2,8192]{2,1,0:T(2,128)(2,1)}), bf16[128,2,8192]{2,1,0:T(2,128)(2,1)}, u32[]{:S(2)}, u32[]{:S(2)}) async-start(bf16[128,2,8192]{2,1,0:T(2,128)(2,1)} %reshape.186), calls=%async_computation.1 | async-start | bytes 8388608 | tf_op jit(solution)/shard_map/all_to_all | solution.py:74
  226.9 43.8 %copy-start.1 = (s32[512]{0:T(512)S(1)}, s32[512]{0:T(512)}, u32[]{:S(2)}) copy-start(s32[512]{0:T(512)} %param.15) | copy-start | bytes 6148
  264.8 66.6 %all-to-all-start.3 = ((bf16[128,2,8192]{2,1,0:T(2,128)(2,1)}), bf16[128,2,8192]{2,1,0:T(2,128)(2,1)}, u32[]{:S(2)}, u32[]{:S(2)}) async-start(bf16[128,2,8192]{2,1,0:T(2,128)(2,1)} %reshape.188), calls=%async_computation.3 | async-start | bytes 8388608 | tf_op jit(solution)/shard_map/all_to_all | solution.py:75
  270.6 256.1 %reduce-scatter.2.cloned.1.call-start = ((), (), s32[]{:S(2)}) async-start(), calls=%async_computation.7 | async-start | bytes 18874368 | tf_op jit(solution)/shard_map/reduce_scatter | solution.py:98
Sparse Core Ops, SparseCore 0:
  91.4 116.0 all-gather.1
  434.0 92.7 reduce-scatter.1
